TPU v7x, 32 devices: a whole 2x2x4 slice. The times are simulated.
32 devices in a mesh: dp: 4 (over z), tensor: 8 (over y, x, core).
Axes of the slice: x: 2, y: 2, z: 4, core: 2. Of those that a mesh axis runs over, the one named last changes fastest.
Arguments:
- gradient: bfloat16 [4, 2560, 8192], P('dp', None, 'tensor'), may hold values from -6 to 6
- feedback: float32 [4, 2560, 8192], P('dp', None, 'tensor'), may hold values from -4 to 4
- q_start: float32 [8192, 32], P('tensor'), may hold values from -6 to 6
Outputs:
- p_factor: float32 [2560, 32], P('tensor')
- q_factor: float32 [8192, 32], P('tensor')
- decoded: float32 [2560, 8192], P(None, 'tensor')
- residual: float32 [4, 2560, 8192], P('dp', None, 'tensor')
All inputs are finite; a program needn't handle non-finite values.
Results may differ from a plain program's by a relative error of at most 0.0003.
Values sent between devices are 32-bit elements; how exact they have to be, the bound alone decides.
A program may use at most 64 MiB of HBM per device.

v0:
```python
import jax
import jax.numpy as jnp
from jax import lax
from jax.sharding import PartitionSpec as P


def orthonormal(p_sum, gram_matrix):
    factor_low = jnp.linalg.cholesky(gram_matrix)
    return jax.scipy.linalg.solve_triangular(factor_low, p_sum.T, lower=True).T


def local(gradient, feedback, q_start):
    high = lax.Precision.HIGHEST
    merged = gradient[0].astype(jnp.float32) + feedback[0]
    row_block = lax.psum_scatter(
        jnp.dot(merged, q_start, precision=high), "tensor", scatter_dimension=0, tiled=True
    )
    row_block = lax.psum(row_block, "dp")
    gram_matrix = lax.psum(jnp.dot(row_block.T, row_block, precision=high), "tensor")
    p_factor = orthonormal(row_block, gram_matrix)
    basis_all = lax.all_gather(p_factor, "tensor", axis=0, tiled=True)
    q_local = lax.dot_general(merged, basis_all, (((0,), (0,)), ((), ())), precision=high)
    q_factor = lax.psum(q_local, "dp") / lax.axis_size("dp")
    decoded = jnp.dot(basis_all, q_factor.T, precision=high)
    residual = merged - decoded
    return (p_factor, q_factor, decoded, residual[None])


def solution(mesh):
    in_specs = (P("dp", None, "tensor"), P("dp", None, "tensor"), P("tensor", None))
    out_specs = (P("tensor", None), P("tensor", None), P(None, "tensor"), P("dp", None, "tensor"))
    return jax.shard_map(local, mesh=mesh, in_specs=in_specs, out_specs=out_specs, check_vma=False)
```

profile of v0, /device:TPU:0, one launch (start us, length us, event | category | flops | bytes accessed | tf_op | source)
XLA Modules:
  0.0 192.3 jit_solution(12324662725646355803)
XLA Ops:
  7.2 0.0 copy-start
  7.2 0.0 reduce-scatter.4.cloned.1.call-start
  7.2 0.8 copy-done
  8.1 12.6 %fusion.2 = f32[2560,32]{1,0:T(8,128)} fusion(f32[1024,32]{0,1:T(8,128)S(1)} %copy-done, f32[1,2560,1024]{2,1,0:T(8,128)} %param.4, bf16[1,2560,1024]{2,1,0:T(8,128)(2,1)} %param.3), kind=kOutput, calls=%fused_computation.3 | convolution fusion | flops 1011875840 | bytes 16187392
  20.7 0.0 reduce-scatter.4.cloned.1.call-update
  20.7 0.0 all-reduce.2.cloned.1.call-start
  20.8 40.0 %reduce-scatter.4.cloned.1.call-done = f32[320,32]{1,0:T(8,128)} async-done(((f32[2560,32]{1,0:T(8,128)}), f32[320,32]{1,0:T(8,128)}) %reduce-scatter.4.cloned.1.call-update) | async-done | bytes 40976
  60.8 1.0 copy.17
  61.8 19.5 %psum.21 = f32[320,32]{0,1:T(8,128)S(1)} all-reduce(f32[320,32]{0,1:T(8,128)S(1)} %copy.17), channel_id=1, replica_groups=mesh['dp'=4,'tensor'=8] {'dp'}, use_global_device_ids=true, to_apply=%region_1.0 | all-reduce | flops 10240 | bytes 81920 | tf_op jit(solution)/shard_map/psum | solution.py:18
  81.3 0.2 fusion.9
  81.5 22.3 %psum.22 = f32[32,32]{0,1:T(8,128)S(1)} all-reduce(f32[32,32]{0,1:T(8,128)S(1)} %fusion.9), channel_id=1, replica_groups=mesh['dp'=4,'tensor'=8] {'tensor'}, use_global_device_ids=true, to_apply=%region_2.0 | all-reduce | flops 1024 | bytes 8192 | tf_op jit(solution)/shard_map/psum | solution.py:19
  103.8 0.1 copy.13
  103.9 2.9 %cholesky.16 = f32[32,32]{1,0:T(8,128)S(1)} custom-call(f32[32,32]{1,0:T(8,128)S(1)} %fusion.8), custom_call_target="Cholesky" | custom-call | tf_op jit(solution)/shard_map/jit(cholesky)/cholesky | solution.py:8
  106.8 0.6 compare_reduce_fusion
  107.5 0.7 fusion.5
  108.1 2.4 %custom-call.7 = f32[1,32,32]{1,2,0:T(8,128)S(1)} custom-call(f32[1,32,32]{2,1,0:T(8,128)S(1)} %fusion.5), custom_call_target="InvertDiagBlocksLowerTriangular" | custom-call | tf_op jit(solution)/shard_map/jit(_solve_triangular)/triangular_solve | solution.py:9
  110.6 0.3 fusion.6
  110.9 0.0 copy-start.3
  110.9 9.6 %all-gather = f32[8,320,32]{1,2,0:T(8,128)S(1)} all-gather(f32[1,320,32]{1,2,0:T(8,128)S(1)} %bitcast.32), channel_id=1, replica_groups=mesh['dp'=4,'tensor'=8] {'tensor'}, dimensions={0}, use_global_device_ids=true | all-gather | bytes 368640 | tf_op jit(solution)/shard_map/all_gather | solution.py:21
  120.4 0.2 copy.14
  120.7 0.1 reshape.21
  120.8 11.0 %fusion = f32[1024,32]{0,1:T(8,128)} fusion(f32[2560,32]{0,1:T(8,128)S(1)} %reshape.21, f32[1,2560,1024]{2,1,0:T(8,128)} %param.4, bf16[1,2560,1024]{2,1,0:T(8,128)(2,1)} %param.3), kind=kOutput, calls=%fused_computation.1 | convolution fusion | flops 1011875840 | bytes 16187392 | tf_op jit(solution)/shard_map/dot_general | solution.py:22
  131.8 0.0 slice-start
  131.8 0.0 all-reduce.2.cloned.1.call-update
  131.8 32.1 %all-reduce.2.cloned.1.call-done = f32[1024,32]{0,1:T(8,128)} async-done(((f32[1024,32]{0,1:T(8,128)}), f32[1024,32]{0,1:T(8,128)}) %all-reduce.2.cloned.1.call-update) | async-done | bytes 131088 | tf_op jit(solution)/shard_map/psum | solution.py:23
  163.9 0.9 broadcast_multiply_fusion
  164.8 0.0 copy-start.2
  164.8 0.0 slice-start.1
  164.8 8.5 %fusion.10 = f32[2560,1024]{1,0:T(8,128)S(1)} fusion(f32[2560,32]{0,1:T(8,128)S(1)} %reshape.21, f32[1024,32]{0,1:T(8,128)S(1)} %broadcast_multiply_fusion), kind=kOutput, calls=%fused_computation.19 | convolution fusion | flops 1006632960 | bytes 10944512 | tf_op jit(solution)/shard_map/dot_general | solution.py:24
  173.3 0.0 copy-done.3
  173.4 0.0 slice-done
  173.4 0.0 slice-done.1
  173.4 0.0 copy-start.1
  173.4 12.1 %fusion.4 = f32[1,2560,1024]{2,1,0:T(8,128)} fusion(f32[2560,1024]{1,0:T(8,128)S(1)} %fusion.10, f32[1,2560,1024]{2,1,0:T(8,128)} %param.4, bf16[1,2560,1024]{2,1,0:T(8,128)(2,1)S(1)} %bitcast.31), kind=kLoop, calls=%fused_computation.5 | loop fusion | flops 7864320 | bytes 36700160 | tf_op jit(solution)/shard_map/broadcast_in_dim | solution.py:26
  185.5 0.0 copy-done.2
  185.5 0.0 copy-done.1
  (3 shorter events, 0.0 us)
Async XLA Ops:
  7.2 0.9 copy-start
  7.2 53.6 %reduce-scatter.4.cloned.1.call-start = ((), (), s32[]{:S(2)}) async-start(), calls=%async_computation.2 | async-start | bytes 1474560
  20.7 143.1 %all-reduce.2.cloned.1.call-start = ((), (), s32[]{:S(2)}) async-start(), calls=%async_computation.1 | async-start | bytes 262144 | tf_op jit(solution)/shard_map/psum | solution.py:23
  110.9 62.5 %copy-start.3 = (f32[320,32]{0,1:T(8,128)}, f32[320,32]{0,1:T(8,128)S(1)}, u32[]{:S(2)}) copy-start(f32[320,32]{0,1:T(8,128)S(1)} %fusion.6) | copy-start | bytes 122884
  131.8 41.6 %slice-start = ((s8[5242880]{0:T(1024)(128)(4,1)}), s8[1048576]{0:T(1024)(128)(4,1)S(1)}, s32[]{:S(2)}) async-start(s8[5242880]{0:T(1024)(128)(4,1)} %bitcast.30), calls=%async_computation.3 | async-start | bytes 2097152
  164.8 20.7 %copy-start.2 = (f32[1024,32]{0,1:T(8,128)}, f32[1024,32]{0,1:T(8,128)S(1)}, u32[]{:S(2)}) copy-start(f32[1024,32]{0,1:T(8,128)S(1)} %broadcast_multiply_fusion) | copy-start | bytes 393220
  164.8 8.6 %slice-start.1 = ((s8[5242880]{0:T(1024)(128)(4,1)}), s8[4194304]{0:T(1024)(128)(4,1)S(1)}, s32[]{:S(2)}) async-start(s8[5242880]{0:T(1024)(128)(4,1)} %bitcast.30), calls=%async_computation.4 | async-start | bytes 8388608
  173.4 12.1 %copy-start.1 = (f32[2560,1024]{1,0:T(8,128)}, f32[2560,1024]{1,0:T(8,128)S(1)}, u32[]{:S(2)}) copy-start(f32[2560,1024]{1,0:T(8,128)S(1)} %fusion.10) | copy-start | bytes 31457284
Sparse Core Ops, SparseCore 0:
  20.9 39.8 reduce-scatter.3
  131.9 31.8 all-reduce.1
where the time goes:
time: 193 us; the launch traced here: 192 us
  waiting for transfers between devices  72.1 us (37%)
  blocking collectives  51.4 us (27%)
  matrix products  32.6 us (17%)
  other arithmetic  19.7 us (10%)
  between operations  14.2 us (7%)
  local copies, waits for them, and re-layouts  2.32 us (1%)
    unnamed x3, waiting for transfers between devices  40 us
    psum x1, waiting for transfers between devices, local(): q_factor = lax.psum(q_local, 'dp') / lax.axis_size('dp')  32.1 us
    psum x1, blocking collectives, local(): lax.psum(jnp.dot(row_block.T, row_block, precision=high), 'tensor')  22.3 us
    psum x1, blocking collectives, local(): row_block = lax.psum(row_block, 'dp')  19.5 us
    unnamed x1, matrix products  12.6 us
    broadcast_in_dim x1, other arithmetic, local(): return (p_factor, q_factor, decoded, residual[None])  12.1 us
    dot_general x1, matrix products, local(): lax.dot_general(merged, basis_all, (((0,), (0,)), ((), ())), precision=high)  11 us
    all_gather x1, blocking collectives, local(): basis_all = lax.all_gather(p_factor, 'tensor', axis=0, tiled=True)  9.56 us
  transfers between devices with their start and end apart: 2, of which 2 were waited for; matrix products, arithmetic and copies ran while one was open for 0% of the time, Pallas kernels for 0%

commit v1 on v0

--- a/solution.py
+++ b/solution.py
@@ -1,7 +1,15 @@
+import functools
 import jax
 import jax.numpy as jnp
 from jax import lax
 from jax.sharding import PartitionSpec as P
+
+
+def detail_ranges(payload, row_axis):
+    return lax.all_gather(payload, axis_name=row_axis).sum(axis=0)
+
+
+roads_arrange = functools.partial(detail_ranges, row_axis="dp")
 
 
 def orthonormal(p_sum, gram_matrix):
@@ -20,7 +28,7 @@
     p_factor = orthonormal(row_block, gram_matrix)
     basis_all = lax.all_gather(p_factor, "tensor", axis=0, tiled=True)
     q_local = lax.dot_general(merged, basis_all, (((0,), (0,)), ((), ())), precision=high)
-    q_factor = lax.psum(q_local, "dp") / lax.axis_size("dp")
+    q_factor = roads_arrange(q_local) / lax.axis_size("dp")
     decoded = jnp.dot(basis_all, q_factor.T, precision=high)
     residual = merged - decoded
     return (p_factor, q_factor, decoded, residual[None])

time: 193 us -> 175 us (0.907)
  waiting for transfers between devices: 72.1 us -> 40.1 us
  blocking collectives: 51.4 us -> 67.8 us
  other arithmetic: 19.7 us -> 17.6 us
    psum x1 -> x0, waiting for transfers between devices: 32.1 us -> none  [local(): q_factor = lax.psum(q_local, 'dp') / lax.axis_size('dp')]
    all_gather x0 -> x1, blocking collectives: none -> 16.5 us  [detail_ranges(): return lax.all_gather(payload, axis_name=row_axis).sum(axis=0)]
    broadcast_in_dim x1, other arithmetic: 12.1 us -> 9.55 us  [local(): return (p_factor, q_factor, decoded, residual[None])]
    unnamed x3 -> x2, waiting for transfers between devices: 40 us -> 40.1 us
  transfers between devices with their start and end apart: 2 -> 1, of which waited for: 2 -> 1; matrix products, arithmetic and copies ran while one was open for 0% -> 0% of each run, Pallas kernels for 0% -> 0%
where the time goes in v1:
time: 175 us
  blocking collectives  67.8 us (39%)
  waiting for transfers between devices  40.1 us (23%)
  matrix products  31.8 us (18%)
  other arithmetic  17.6 us (10%)
  between operations  14.2 us (8%)
  local copies, waits for them, and re-layouts  3.47 us (2%)
    unnamed x2, waiting for transfers between devices  40.1 us
    psum x1, blocking collectives, local(): lax.psum(jnp.dot(row_block.T, row_block, precision=high), 'tensor')  22.3 us
    psum x1, blocking collectives, local(): row_block = lax.psum(row_block, 'dp')  19.5 us
    all_gather x1, blocking collectives, detail_ranges(): return lax.all_gather(payload, axis_name=row_axis).sum(axis=0)  16.5 us
    unnamed x1, matrix products  12.6 us
    dot_general x1, matrix products, local(): lax.dot_general(merged, basis_all, (((0,), (0,)), ((), ())), precision=high)  10.2 us
    all_gather x1, blocking collectives, local(): basis_all = lax.all_gather(p_factor, 'tensor', axis=0, tiled=True)  9.56 us
    broadcast_in_dim x1, other arithmetic, local(): return (p_factor, q_factor, decoded, residual[None])  9.55 us
  transfers between devices with their start and end apart: 1, of which 1 were waited for; matrix products, arithmetic and copies ran while one was open for 0% of the time, Pallas kernels for 0%

profile of v1, /device:TPU:0, one launch (start us, length us, event | category | flops | bytes accessed | tf_op | source)
XLA Modules:
  0.0 175.0 jit_solution(8001131151419898893)
XLA Ops:
  7.2 0.0 copy-start
  7.2 0.0 reduce-scatter.4.cloned.1.call-start
  7.2 0.8 copy-done
  8.1 12.6 %fusion.2 = f32[2560,32]{1,0:T(8,128)} fusion(f32[1024,32]{0,1:T(8,128)S(1)} %copy-done, f32[1,2560,1024]{2,1,0:T(8,128)} %param.4, bf16[1,2560,1024]{2,1,0:T(8,128)(2,1)} %param.3), kind=kOutput, calls=%fused_computation.3 | convolution fusion | flops 1011875840 | bytes 16187392
  20.7 0.0 reduce-scatter.4.cloned.1.call-update
  20.7 40.0 %reduce-scatter.4.cloned.1.call-done = f32[320,32]{1,0:T(8,128)} async-done(((f32[2560,32]{1,0:T(8,128)}), f32[320,32]{1,0:T(8,128)}) %reduce-scatter.4.cloned.1.call-update) | async-done | bytes 40976
  60.8 1.0 copy.17
  61.8 19.5 %psum.14 = f32[320,32]{0,1:T(8,128)S(1)} all-reduce(f32[320,32]{0,1:T(8,128)S(1)} %copy.17), channel_id=1, replica_groups=mesh['dp'=4,'tensor'=8] {'dp'}, use_global_device_ids=true, to_apply=%region_1.0 | all-reduce | flops 10240 | bytes 81920 | tf_op jit(solution)/shard_map/psum | solution.py:26
  81.3 0.2 fusion.9
  81.5 22.3 %psum.15 = f32[32,32]{0,1:T(8,128)S(1)} all-reduce(f32[32,32]{0,1:T(8,128)S(1)} %fusion.9), channel_id=1, replica_groups=mesh['dp'=4,'tensor'=8] {'tensor'}, use_global_device_ids=true, to_apply=%region_2.0 | all-reduce | flops 1024 | bytes 8192 | tf_op jit(solution)/shard_map/psum | solution.py:27
  103.8 0.1 copy.13
  103.9 2.9 %cholesky.16 = f32[32,32]{1,0:T(8,128)S(1)} custom-call(f32[32,32]{1,0:T(8,128)S(1)} %fusion.8), custom_call_target="Cholesky" | custom-call | tf_op jit(solution)/shard_map/jit(cholesky)/cholesky | solution.py:16
  106.8 0.6 compare_reduce_fusion
  107.5 0.7 fusion.5
  108.1 2.4 %custom-call.7 = f32[1,32,32]{1,2,0:T(8,128)S(1)} custom-call(f32[1,32,32]{2,1,0:T(8,128)S(1)} %fusion.5), custom_call_target="InvertDiagBlocksLowerTriangular" | custom-call | tf_op jit(solution)/shard_map/jit(_solve_triangular)/triangular_solve | solution.py:17
  110.6 0.3 fusion.6
  110.9 0.0 copy-start.3
  110.9 9.6 %all-gather.1 = f32[8,320,32]{1,2,0:T(8,128)S(1)} all-gather(f32[1,320,32]{1,2,0:T(8,128)S(1)} %bitcast.34), channel_id=1, replica_groups=mesh['dp'=4,'tensor'=8] {'tensor'}, dimensions={0}, use_global_device_ids=true | all-gather | bytes 368640 | tf_op jit(solution)/shard_map/all_gather | solution.py:29
  120.4 0.2 copy.14
  120.7 0.1 reshape.22
  120.8 10.2 %fusion = f32[1024,32]{0,1:T(8,128)S(1)} fusion(f32[2560,32]{0,1:T(8,128)S(1)} %reshape.22, f32[1,2560,1024]{2,1,0:T(8,128)} %param.4, bf16[1,2560,1024]{2,1,0:T(8,128)(2,1)} %param.3), kind=kOutput, calls=%fused_computation.1 | convolution fusion | flops 1011875840 | bytes 16187392 | tf_op jit(solution)/shard_map/dot_general | solution.py:30
  131.0 0.0 slice-start
  131.0 16.5 %all-gather = f32[4096,32]{0,1:T(8,128)S(1)} all-gather(f32[1024,32]{0,1:T(8,128)S(1)} %fusion), channel_id=2, replica_groups=mesh['dp'=4,'tensor'=8] {'dp'}, dimensions={0}, use_global_device_ids=true | all-gather | bytes 655360 | tf_op jit(solution)/shard_map/all_gather | solution.py:9
  147.4 1.1 reshape.20
  148.6 1.4 reduce_sum.9
  150.0 0.0 copy-start.2
  150.0 0.0 slice-start.1
  150.0 0.0 slice-start.2
  150.0 8.5 %fusion.10 = f32[2560,1024]{1,0:T(8,128)S(1)} fusion(f32[2560,32]{0,1:T(8,128)S(1)} %reshape.22, f32[1024,32]{0,1:T(8,128)S(1)} %broadcast_multiply_fusion), kind=kOutput, calls=%fused_computation.19 | convolution fusion | flops 1006632960 | bytes 10944512 | tf_op jit(solution)/shard_map/dot_general | solution.py:32
  158.6 0.0 copy-done.3
  158.6 0.0 slice-done
  158.6 0.0 slice-done.1
  158.6 0.0 slice-done.2
  158.6 0.0 copy-start.1
  158.6 9.5 %fusion.4 = f32[1,2560,1024]{2,1,0:T(8,128)} fusion(f32[2560,1024]{1,0:T(8,128)S(1)} %fusion.10, f32[1,2560,1024]{2,1,0:T(8,128)S(1)} %bitcast.33, bf16[1,2560,1024]{2,1,0:T(8,128)(2,1)} %param.3), kind=kLoop, calls=%fused_computation.5 | loop fusion | flops 7864320 | bytes 36700160 | tf_op jit(solution)/shard_map/broadcast_in_dim | solution.py:34
  168.2 0.0 copy-done.2
  168.2 0.0 copy-done.1
  (4 shorter events, 0.1 us)
Async XLA Ops:
  7.2 0.9 copy-start
  7.2 53.6 %reduce-scatter.4.cloned.1.call-start = ((), (), s32[]{:S(2)}) async-start(), calls=%async_computation.1 | async-start | bytes 1474560
  110.9 47.7 %copy-start.3 = (f32[320,32]{0,1:T(8,128)}, f32[320,32]{0,1:T(8,128)S(1)}, u32[]{:S(2)}) copy-start(f32[320,32]{0,1:T(8,128)S(1)} %fusion.6) | copy-start | bytes 122884
  131.0 27.6 %slice-start = ((s8[10485760]{0:T(1024)(128)(4,1)}), s8[2097152]{0:T(1024)(128)(4,1)S(1)}, s32[]{:S(2)}) async-start(s8[10485760]{0:T(1024)(128)(4,1)} %bitcast.32), calls=%async_computation.2 | async-start | bytes 4194304
  150.0 18.2 %copy-start.2 = (f32[1024,32]{0,1:T(8,128)}, f32[1024,32]{0,1:T(8,128)S(1)}, u32[]{:S(2)}) copy-start(f32[1024,32]{0,1:T(8,128)S(1)} %broadcast_multiply_fusion) | copy-start | bytes 393220
  150.0 8.6 %slice-start.1 = ((s8[10485760]{0:T(1024)(128)(4,1)}), s8[4194304]{0:T(1024)(128)(4,1)S(1)}, s32[]{:S(2)}) async-start(s8[10485760]{0:T(1024)(128)(4,1)} %bitcast.32), calls=%async_computation.3 | async-start | bytes 8388608
  150.0 8.6 %slice-start.2 = ((s8[10485760]{0:T(1024)(128)(4,1)}), s8[4194304]{0:T(1024)(128)(4,1)S(1)}, s32[]{:S(2)}) async-start(s8[10485760]{0:T(1024)(128)(4,1)} %bitcast.32), calls=%async_computation.4 | async-start | bytes 8388608
  158.6 9.6 %copy-start.1 = (f32[2560,1024]{1,0:T(8,128)}, f32[2560,1024]{1,0:T(8,128)S(1)}, u32[]{:S(2)}) copy-start(f32[2560,1024]{1,0:T(8,128)S(1)} %fusion.10) | copy-start | bytes 31457284
Sparse Core Ops, SparseCore 0:
  20.9 39.8 reduce-scatter.3
